TPU v7x, 32 devices: a whole 2x2x4 slice. The times are simulated.
32 devices in a mesh: lat: 4 (over z), lon: 4 (over y, x), obs: 2 (over core).
Axes of the slice: x: 2, y: 2, z: 4, core: 2. Of those that a mesh axis runs over, the one named last changes fastest.
Arguments:
- innovation: float32 [4096, 128], P(('lat', 'lon', 'obs')), may hold values from -6 to 6
- obs_error: float32 [4096, 128], P(('lat', 'lon', 'obs')), may hold values from 0.5 to 2
- obs_offset: float32 [2, 4096, 128], P(None, ('lat', 'lon', 'obs')), may hold values from 0 to 1
- obs_cell: int32 [4096, 128], P(('lat', 'lon', 'obs')), may hold values from 0 to 65535
- obs_owner: int32 [32, 128], P(('lat', 'lon', 'obs')), may hold values from 0 to 15, as said below
- block_count: int32 [32], P(('lat', 'lon', 'obs')), may hold values from 64 to 128
- land_mask: int32 [256, 4096], P(('lat', 'obs'), 'lon'), may hold values from 0 to 1, as said below
- inertia: float32 [256, 4096], P(('lat', 'obs'), 'lon'), may hold values from 0.002 to 0.05
- sea_depth: float32 [256, 4096], P(('lat', 'obs'), 'lon'), may hold values from 0.5 to 5
Outputs:
- adjoint_field: float32 [256, 4096], P(('lat', 'obs'), 'lon')
- residual: float32 [256, 4096], P(('lat', 'obs'), 'lon')
Inputs may be any that keep to these rules, and one draw needn't show every extreme that they name: `obs_owner`: among the live blocks of one device at most 16 name the same tile; in every draw some tile is named by exactly 16 live blocks of every device. `land_mask`: the first and the last grid row are land.
All inputs are finite; a program needn't handle non-finite values.
Results may differ from a plain program's by a relative error of at most 0.0003.
Values sent between devices are 32-bit elements; how exact they have to be, the bound alone decides.
A program may use at most 64 MiB of HBM per device.

v0:
```python
import jax
import jax.numpy as jnp
from jax import lax
from jax.sharding import PartitionSpec as P

ITERS = 5


def extended(block, sides, width):
    for axis, dim in sides:
        count = lax.axis_size(axis)
        forward = [(i, i + 1) for i in range(count - 1)]
        forward.append((count - 1, 0))
        backward = [(target, source) for source, target in forward]
        low = lax.ppermute(
            lax.slice_in_dim(block, block.shape[dim] - width, None, axis=dim), axis, forward
        )
        high = lax.ppermute(lax.slice_in_dim(block, 0, width, axis=dim), axis, backward)
        block = jnp.concatenate([low, block, high], axis=dim)
    return block


def shifted(value, axis, steps):
    count = lax.axis_size(axis)
    pairs = [(source, (source + steps) % count) for source in range(count)]
    return lax.ppermute(value, axis, pairs)


def shifted_2(block, axis, distance):
    devices = range(lax.axis_size(axis))
    route = [(i - distance, i) for i in devices if i - distance in devices]
    return lax.ppermute(block, axis, route)


def border(field):
    return extended(field, ((("lat", "obs"), 0), ("lon", 1)), 1)


def two_products(residual, applied):
    return lax.psum(
        (jnp.sum(residual * residual), jnp.sum(residual * applied)), ("lat", "lon", "obs")
    )


def body(
    innovation,
    obs_error,
    obs_offset,
    obs_cell,
    obs_owner,
    block_count,
    land_mask,
    inertia,
    sea_depth,
):
    block_total = obs_owner.shape[1]
    block_width = innovation.shape[1]
    n_lat = lax.axis_size("lat")
    n_lon = lax.axis_size("lon")
    tile_count = n_lat * n_lon
    capacity = max(3, 2 * ((block_total + tile_count - 1) // tile_count))
    slot_total = tile_count * capacity
    tile_rows = land_mask.shape[0] * lax.axis_size("obs")
    tile_cols = land_mask.shape[1]
    owners = obs_owner[0]
    block_ids = jnp.arange(block_total)
    is_live = block_ids < block_count[0]
    earlier = block_ids[None, :] < block_ids[:, None]
    same_owner = (owners[None, :] == owners[:, None]) & earlier & is_live[None, :]
    slot_rank = jnp.sum(same_owner.astype(jnp.int32), axis=1)
    target = jnp.where(is_live, owners * capacity + slot_rank, slot_total)
    scaled = innovation / (obs_error * obs_error)
    floats = jnp.stack([scaled, obs_offset[0], obs_offset[1]], axis=1)

    def put_slots(values):
        holder = jnp.zeros((slot_total + 1,) + values.shape[1:], values.dtype)
        return holder.at[target].set(values)[:slot_total]

    sent_floats = put_slots(floats)
    sent_cells = put_slots(obs_cell)
    received, cell_ids = (
        lax.all_to_all(
            sent_floats.reshape(tile_count, capacity, 3, block_width),
            ("lat", "lon"),
            split_axis=0,
            concat_axis=0,
            tiled=True,
        ),
        lax.all_to_all(
            sent_cells.reshape(tile_count, capacity, block_width),
            ("lat", "lon"),
            split_axis=0,
            concat_axis=0,
            tiled=True,
        ),
    )
    received = received.reshape(-1, 3, block_width)
    cell_ids = cell_ids.reshape(-1, block_width)
    group = 1
    for size_try in range(1, slot_total + 1):
        if slot_total % size_try == 0 and size_try * block_width <= 4096:
            group = size_try
    turns = slot_total // group
    group_obs = group * block_width
    scaled_in = received[:, 0].reshape(turns, group_obs)
    north_frac = received[:, 1].reshape(turns, group_obs)
    east_frac = received[:, 2].reshape(turns, group_obs)
    cells_in = cell_ids.reshape(turns, group_obs)
    wide = tile_cols + 1
    row_axis = jnp.arange(tile_rows + 1, dtype=jnp.int32)[:, None]
    col_axis = jnp.arange(wide, dtype=jnp.int32)[None, :]

    def spread(total, pieces):
        amount, north, east, cells = pieces
        cell_row = (cells // tile_cols)[None, :]
        cell_col = (cells % tile_cols)[:, None]
        row_weights = (
            jnp.where(row_axis == cell_row, 1.0 - north[None, :], 0.0)
            + jnp.where(row_axis == cell_row + 1, north[None, :], 0.0)
        ) * amount[None, :]
        col_weights = jnp.where(col_axis == cell_col, 1.0 - east[:, None], 0.0) + jnp.where(
            col_axis == cell_col + 1, east[:, None], 0.0
        )
        return (
            total
            + jnp.dot(
                row_weights,
                col_weights,
                precision=lax.Precision.HIGHEST,
                preferred_element_type=jnp.float32,
            ),
            None,
        )

    partial_value, unused = lax.scan(
        spread,
        jnp.zeros((tile_rows + 1, wide), jnp.float32),
        (scaled_in, north_frac, east_frac, cells_in),
    )
    arrived_col = shifted(partial_value[:, tile_cols], "lon", 1)
    partial_value = partial_value[:, :tile_cols].at[:, 0].add(arrived_col)
    arrived_row = shifted_2(partial_value[tile_rows], "lat", 1)
    tile_part = partial_value[:tile_rows].at[0].add(arrived_row)
    ocean = land_mask.astype(jnp.float32)
    forcing = lax.psum_scatter(tile_part, "obs", scatter_dimension=0, tiled=True) * ocean
    conduct = ocean * sea_depth
    padded = border(conduct)
    cond_north = jnp.sqrt(conduct * padded[:-2, 1:-1])
    cond_south = jnp.sqrt(conduct * padded[2:, 1:-1])
    cond_west = jnp.sqrt(conduct * padded[1:-1, :-2])
    cond_east = jnp.sqrt(conduct * padded[1:-1, 2:])
    diagonal = inertia + cond_north + cond_south + cond_west + cond_east

    def operate(field):
        outer = border(field)
        return (
            diagonal * field
            - cond_north * outer[:-2, 1:-1]
            - cond_south * outer[2:, 1:-1]
            - cond_west * outer[1:-1, :-2]
            - cond_east * outer[1:-1, 2:]
        )

    adjoint_field = jnp.zeros_like(forcing)
    residual = forcing
    applied = operate(residual)
    norm_now, product = two_products(residual, applied)
    step_size = norm_now / product
    direction = residual
    applied_dir = applied
    for iteration in range(ITERS):
        adjoint_field = adjoint_field + step_size * direction
        residual = residual - step_size * applied_dir
        if iteration + 1 < ITERS:
            applied = operate(residual)
            norm_next, product = two_products(residual, applied)
            beta_ratio = norm_next / norm_now
            step_size = norm_next / (product - beta_ratio * norm_next / step_size)
            direction = residual + beta_ratio * direction
            applied_dir = applied + beta_ratio * applied_dir
            norm_now = norm_next
    return (adjoint_field, residual)


def solution(mesh):
    in_specs = (
        P(("lat", "lon", "obs"), None),
        P(("lat", "lon", "obs"), None),
        P(None, ("lat", "lon", "obs"), None),
        P(("lat", "lon", "obs"), None),
        P(("lat", "lon", "obs"), None),
        P(("lat", "lon", "obs")),
        P(("lat", "obs"), "lon"),
        P(("lat", "obs"), "lon"),
        P(("lat", "obs"), "lon"),
    )
    out_specs = (P(("lat", "obs"), "lon"), P(("lat", "obs"), "lon"))
    return jax.shard_map(body, mesh=mesh, in_specs=in_specs, out_specs=out_specs, check_vma=False)
```

profile of v0, /device:TPU:14, one launch (start us, length us, event | category | flops | bytes accessed | tf_op | source)
XLA Modules:
  0.0 499.8 jit_solution(3898041280866517940)
XLA Ops:
  11.3 7.1 %all-to-all-start = ((s32[16,16,128]{2,1,0:T(8,128)}), s32[16,16,128]{2,1,0:T(8,128)S(1)}, u32[]{:S(2)}, u32[]{:S(2)}) async-start(s32[16,16,128]{2,1,0:T(8,128)} %bitcast.5), calls=%async_computation | async-start | bytes 262144 | tf_op jit(solution)/shard_map/all_to_all | solution.py:89
  18.8 4.4 scatter_fusion
  24.0 7.0 %all-to-all-start.1 = ((f32[16,16,3,128]{3,1,2,0:T(8,128)}), f32[16,16,3,128]{3,1,2,0:T(8,128)S(1)}, u32[]{:S(2)}, u32[]{:S(2)}) async-start(f32[16,16,3,128]{3,1,2,0:T(8,128)} %copy.29), calls=%async_computation.1 | async-start | bytes 786432 | tf_op jit(solution)/shard_map/all_to_all | solution.py:82
  31.1 9.6 %all-to-all-done.1 = f32[16,16,3,128]{3,1,2,0:T(8,128)S(1)} async-done(((f32[16,16,3,128]{3,1,2,0:T(8,128)}), f32[16,16,3,128]{3,1,2,0:T(8,128)S(1)}, u32[]{:S(2)}, u32[]{:S(2)}) %all-to-all-start.1) | async-done | bytes 393248 | tf_op jit(solution)/shard_map/all_to_all | solution.py:82
  40.9 152.0 %while.16 = (s32[]{:T(128)}, f32[65,1025]{1,0:T(8,128)S(1)}, s32[8,4096]{1,0:T(8,128)S(1)}, f32[8,4096]{1,0:T(8,128)S(1)}, f32[8,4096]{1,0:T(8,128)S(1)}, /*index=5*/f32[8,4096]{1,0:T(8,128)S(1)}, s32[]{:T(128)}, s32[]{:T(128)}) while((s32[]{:T(128)}, f32[65,1025]{1,0:T(8,128)S(1)}, s32[8,4096]{1,0:T(8,128)S(1)}, ...), condition=%wide.region_4.5_spmd.clone.clone, body=%wide.region_3.4_spmd.clone.clone.sunk | while | flops 3297597440 | bytes 942707 | solution.py:135
  41.1 18.7 %fusion.98 = f32[65,1025]{1,0:T(8,128)S(1)} fusion(f32[4096]{0:T(1024)S(1)} %bitcast.58, s32[4096]{0:T(1024)S(1)} %get-tuple-element.312, f32[4096]{0:T(1024)S(1)} %broadcast_subtract_fusion.5, s32[4096]{0:T(1024)S(1)} %get-tuple-element.313, f32[4096]{0:T(1024)S(1)} %bitcast.63, f32[4096]{0:T(1024)S(1)} %bitcast.62, s32[4096]{0:T(1024)S(1)} %bitcast.64, ...), kind=kOutput, calls=%fused_computation.15.clone.1 | convolution fusion | flops 3297474560 | bytes 680457 | tf_op jit(solution)/shard_map/while/body/eval_jaxpr/dot_general | solution.py:126
  60.1 18.7 %fusion.98 = f32[65,1025]{1,0:T(8,128)S(1)} fusion(f32[4096]{0:T(1024)S(1)} %bitcast.58, s32[4096]{0:T(1024)S(1)} %get-tuple-element.312, f32[4096]{0:T(1024)S(1)} %broadcast_subtract_fusion.5, s32[4096]{0:T(1024)S(1)} %get-tuple-element.313, f32[4096]{0:T(1024)S(1)} %bitcast.63, f32[4096]{0:T(1024)S(1)} %bitcast.62, s32[4096]{0:T(1024)S(1)} %bitcast.64, ...), kind=kOutput, calls=%fused_computation.15.clone.1 | convolution fusion | flops 3297474560 | bytes 680457 | tf_op jit(solution)/shard_map/while/body/eval_jaxpr/dot_general | solution.py:126
  79.1 18.7 %fusion.98 = f32[65,1025]{1,0:T(8,128)S(1)} fusion(f32[4096]{0:T(1024)S(1)} %bitcast.58, s32[4096]{0:T(1024)S(1)} %get-tuple-element.312, f32[4096]{0:T(1024)S(1)} %broadcast_subtract_fusion.5, s32[4096]{0:T(1024)S(1)} %get-tuple-element.313, f32[4096]{0:T(1024)S(1)} %bitcast.63, f32[4096]{0:T(1024)S(1)} %bitcast.62, s32[4096]{0:T(1024)S(1)} %bitcast.64, ...), kind=kOutput, calls=%fused_computation.15.clone.1 | convolution fusion | flops 3297474560 | bytes 680457 | tf_op jit(solution)/shard_map/while/body/eval_jaxpr/dot_general | solution.py:126
  98.1 18.7 %fusion.98 = f32[65,1025]{1,0:T(8,128)S(1)} fusion(f32[4096]{0:T(1024)S(1)} %bitcast.58, s32[4096]{0:T(1024)S(1)} %get-tuple-element.312, f32[4096]{0:T(1024)S(1)} %broadcast_subtract_fusion.5, s32[4096]{0:T(1024)S(1)} %get-tuple-element.313, f32[4096]{0:T(1024)S(1)} %bitcast.63, f32[4096]{0:T(1024)S(1)} %bitcast.62, s32[4096]{0:T(1024)S(1)} %bitcast.64, ...), kind=kOutput, calls=%fused_computation.15.clone.1 | convolution fusion | flops 3297474560 | bytes 680457 | tf_op jit(solution)/shard_map/while/body/eval_jaxpr/dot_general | solution.py:126
  117.1 18.7 %fusion.98 = f32[65,1025]{1,0:T(8,128)S(1)} fusion(f32[4096]{0:T(1024)S(1)} %bitcast.58, s32[4096]{0:T(1024)S(1)} %get-tuple-element.312, f32[4096]{0:T(1024)S(1)} %broadcast_subtract_fusion.5, s32[4096]{0:T(1024)S(1)} %get-tuple-element.313, f32[4096]{0:T(1024)S(1)} %bitcast.63, f32[4096]{0:T(1024)S(1)} %bitcast.62, s32[4096]{0:T(1024)S(1)} %bitcast.64, ...), kind=kOutput, calls=%fused_computation.15.clone.1 | convolution fusion | flops 3297474560 | bytes 680457 | tf_op jit(solution)/shard_map/while/body/eval_jaxpr/dot_general | solution.py:126
  136.0 18.7 %fusion.98 = f32[65,1025]{1,0:T(8,128)S(1)} fusion(f32[4096]{0:T(1024)S(1)} %bitcast.58, s32[4096]{0:T(1024)S(1)} %get-tuple-element.312, f32[4096]{0:T(1024)S(1)} %broadcast_subtract_fusion.5, s32[4096]{0:T(1024)S(1)} %get-tuple-element.313, f32[4096]{0:T(1024)S(1)} %bitcast.63, f32[4096]{0:T(1024)S(1)} %bitcast.62, s32[4096]{0:T(1024)S(1)} %bitcast.64, ...), kind=kOutput, calls=%fused_computation.15.clone.1 | convolution fusion | flops 3297474560 | bytes 680457 | tf_op jit(solution)/shard_map/while/body/eval_jaxpr/dot_general | solution.py:126
  155.0 18.7 %fusion.98 = f32[65,1025]{1,0:T(8,128)S(1)} fusion(f32[4096]{0:T(1024)S(1)} %bitcast.58, s32[4096]{0:T(1024)S(1)} %get-tuple-element.312, f32[4096]{0:T(1024)S(1)} %broadcast_subtract_fusion.5, s32[4096]{0:T(1024)S(1)} %get-tuple-element.313, f32[4096]{0:T(1024)S(1)} %bitcast.63, f32[4096]{0:T(1024)S(1)} %bitcast.62, s32[4096]{0:T(1024)S(1)} %bitcast.64, ...), kind=kOutput, calls=%fused_computation.15.clone.1 | convolution fusion | flops 3297474560 | bytes 680457 | tf_op jit(solution)/shard_map/while/body/eval_jaxpr/dot_general | solution.py:126
  174.0 18.7 %fusion.98 = f32[65,1025]{1,0:T(8,128)S(1)} fusion(f32[4096]{0:T(1024)S(1)} %bitcast.58, s32[4096]{0:T(1024)S(1)} %get-tuple-element.312, f32[4096]{0:T(1024)S(1)} %broadcast_subtract_fusion.5, s32[4096]{0:T(1024)S(1)} %get-tuple-element.313, f32[4096]{0:T(1024)S(1)} %bitcast.63, f32[4096]{0:T(1024)S(1)} %bitcast.62, s32[4096]{0:T(1024)S(1)} %bitcast.64, ...), kind=kOutput, calls=%fused_computation.15.clone.1 | convolution fusion | flops 3297474560 | bytes 680457 | tf_op jit(solution)/shard_map/while/body/eval_jaxpr/dot_general | solution.py:126
  193.1 2.1 collective-permute-start
  199.6 3.5 collective-permute-done.1
  204.0 8.9 %reduce-scatter.2.cloned.1.call-done = f32[32,1024]{1,0:T(8,128)} async-done(((f32[64,1024]{1,0:T(8,128)}), f32[32,1024]{1,0:T(8,128)}) %reduce-scatter.2.cloned.1.call-update) | async-done | bytes 131088 | tf_op jit(solution)/shard_map/reduce_scatter | solution.py:145
  223.5 2.3 collective-permute-done.9
  226.7 44.0 %all-reduce.4 = (f32[]{:T(128)}, f32[]{:T(128)}) all-reduce(f32[]{:T(128)} %get-tuple-element.194, f32[]{:T(128)} %get-tuple-element.193), channel_id=1, replica_groups=mesh['lat'=4,'lon'=4,'obs'=2] {'lat','lon','obs'}, use_global_device_ids=true, to_apply=%region_8.9 | all-reduce | flops 2 | bytes 16 | tf_op jit(solution)/shard_map/psum | solution.py:40
  275.3 2.0 collective-permute-start.13
  281.0 41.2 %all-reduce.3 = (f32[]{:T(128)}, f32[]{:T(128)}) all-reduce(f32[]{:T(128)} %get-tuple-element.192, f32[]{:T(128)} %get-tuple-element.191), channel_id=1, replica_groups=mesh['lat'=4,'lon'=4,'obs'=2] {'lat','lon','obs'}, use_global_device_ids=true, to_apply=%region_12.13 | all-reduce | flops 2 | bytes 16 | tf_op jit(solution)/shard_map/psum | solution.py:40
  329.9 2.0 collective-permute-start.17
  335.6 42.7 %all-reduce.2 = (f32[]{:T(128)}, f32[]{:T(128)}) all-reduce(f32[]{:T(128)} %get-tuple-element.190, f32[]{:T(128)} %get-tuple-element.189), channel_id=1, replica_groups=mesh['lat'=4,'lon'=4,'obs'=2] {'lat','lon','obs'}, use_global_device_ids=true, to_apply=%region_16.17 | all-reduce | flops 2 | bytes 16 | tf_op jit(solution)/shard_map/psum | solution.py:40
  391.2 41.8 %all-reduce.1 = (f32[]{:T(128)}, f32[]{:T(128)}) all-reduce(f32[]{:T(128)} %get-tuple-element.188, f32[]{:T(128)} %get-tuple-element.187), channel_id=1, replica_groups=mesh['lat'=4,'lon'=4,'obs'=2] {'lat','lon','obs'}, use_global_device_ids=true, to_apply=%region_20.21 | all-reduce | flops 2 | bytes 16 | tf_op jit(solution)/shard_map/psum | solution.py:40
  445.8 42.4 %all-reduce = (f32[]{:T(128)}, f32[]{:T(128)}) all-reduce(f32[]{:T(128)} %get-tuple-element.186, f32[]{:T(128)} %get-tuple-element.185), channel_id=1, replica_groups=mesh['lat'=4,'lon'=4,'obs'=2] {'lat','lon','obs'}, use_global_device_ids=true, to_apply=%region_24.25 | all-reduce | flops 2 | bytes 16 | tf_op jit(solution)/shard_map/psum | solution.py:40
  (157 shorter events, 55.3 us)
Async XLA Ops:
  11.3 12.7 %all-to-all-start = ((s32[16,16,128]{2,1,0:T(8,128)}), s32[16,16,128]{2,1,0:T(8,128)S(1)}, u32[]{:S(2)}, u32[]{:S(2)}) async-start(s32[16,16,128]{2,1,0:T(8,128)} %bitcast.5), calls=%async_computation | async-start | bytes 262144 | tf_op jit(solution)/shard_map/all_to_all | solution.py:89
  24.0 16.7 %all-to-all-start.1 = ((f32[16,16,3,128]{3,1,2,0:T(8,128)}), f32[16,16,3,128]{3,1,2,0:T(8,128)S(1)}, u32[]{:S(2)}, u32[]{:S(2)}) async-start(f32[16,16,3,128]{3,1,2,0:T(8,128)} %copy.29), calls=%async_computation.1 | async-start | bytes 786432 | tf_op jit(solution)/shard_map/all_to_all | solution.py:82
  31.1 181.8 %reduce-scatter.2.cloned.1.call-start = ((), (), s32[]{:S(2)}) async-start(), calls=%async_computation.3 | async-start | bytes 393216 | tf_op jit(solution)/shard_map/reduce_scatter | solution.py:145
  193.1 3.6 collective-permute-start
  197.6 5.5 %collective-permute-start.1 = (f32[1024]{0:T(1024)S(1)}, f32[1024]{0:T(1024)S(1)}, u32[]{:S(2)}, u32[]{:S(2)}) collective-permute-start(f32[1024]{0:T(1024)S(1)} %bitcast.68), channel_id=1, source_target_pairs={{0,8},{8,16},{16,24},{1,9},{9,17},{17,25},{2,10},{10,18},{18,26},{... | collective-permute-start | bytes 12296 | tf_op jit(solution)/shard_map/ppermute | solution.py:32
  213.8 3.6 collective-permute-start.2
  214.2 3.2 collective-permute-start.3
  215.6 3.9 collective-permute-start.6
  215.7 3.9 collective-permute-start.7
  217.5 4.1 collective-permute-start.4
  218.1 4.8 collective-permute-start.5
  219.6 3.9 collective-permute-start.8
  221.1 4.7 collective-permute-start.9
  272.0 3.1 collective-permute-start.10
  275.2 3.8 collective-permute-start.12
  275.3 4.7 collective-permute-start.13
  326.7 3.1 collective-permute-start.14
  329.9 3.8 collective-permute-start.16
  329.9 4.7 collective-permute-start.17
  385.5 3.8 collective-permute-start.20
  385.6 4.7 collective-permute-start.21
  437.0 3.1 collective-permute-start.22
  440.2 3.8 collective-permute-start.24
  440.2 4.7 collective-permute-start.25
  (12 other events, 105.4 us)
Sparse Core Ops, SparseCore 0:
  204.1 8.7 reduce-scatter.1
where the time goes:
time: 501 us; the launch traced here: 500 us
  blocking collectives  212 us (42%)
  matrix products  150 us (30%)
  waiting for transfers between devices  42.9 us (9%)
  starting transfers between devices  41.1 us (8%)
  between operations  32.8 us (7%)
  other arithmetic  11.1 us (2%)
  local copies, waits for them, and re-layouts  9.14 us (2%)
    psum x5, blocking collectives, two_products(): lax.psum((jnp.sum(residual * residual), jnp.sum(residual * applied)), ('l...  212 us
    dot_general x8, matrix products, spread(): jnp.dot(row_weights, col_weights, precision=lax.Precision.HIGHEST, prefer...  150 us
    ppermute x12, starting transfers between devices, extended(): lax.ppermute(lax.slice_in_dim(block, 0, width, axis=dim), axis, backward)  20.2 us
    ppermute x12, waiting for transfers between devices, extended(): lax.ppermute(lax.slice_in_dim(block, block.shape[dim] - width, None, axis...  12.8 us
  transfers between devices with their start and end apart: 29, of which 19 were waited for; matrix products, arithmetic and copies ran while one was open for 1% of the time, Pallas kernels for 0%

commit v1 on v0

--- a/solution.py
+++ b/solution.py
@@ -38,7 +38,7 @@
 
 def two_products(residual, applied):
     return lax.psum(
-        (jnp.sum(residual * residual), jnp.sum(residual * applied)), ("lat", "lon", "obs")
+        lax.psum((jnp.sum(residual * residual), jnp.sum(residual * applied)), ("lon", "obs")), "lat"
     )
 
 

time: 501 us -> 431 us (0.86); the launches traced: 500 us -> 422 us
  blocking collectives: 212 us -> 123 us
  waiting for transfers between devices: 42.9 us -> 50.1 us
    psum x5, blocking collectives: 212 us -> 60.7 us  [two_products(): lax.psum((jnp.sum(residual * residual), jnp.sum(residual * applied)), ('l...]
    psum x0 -> x5, blocking collectives: none -> 62.7 us  [two_products(): lax.psum(lax.psum((jnp.sum(residual * residual), jnp.sum(residual * appli...]
    ppermute x12, starting transfers between devices: 2.7 us -> 13.8 us  [extended(): lax.ppermute(lax.slice_in_dim(block, block.shape[dim] - width, None, axis...]
    ppermute x12, waiting for transfers between devices: 7.43 us -> 15 us  [extended(): lax.ppermute(lax.slice_in_dim(block, 0, width, axis=dim), axis, backward)]
    ppermute x12, starting transfers between devices: 20.2 us -> 12.9 us  [extended(): lax.ppermute(lax.slice_in_dim(block, 0, width, axis=dim), axis, backward)]
  transfers between devices with their start and end apart: 29 -> 29, of which waited for: 19 -> 19; matrix products, arithmetic and copies ran while one was open for 1% -> 2% of each run, Pallas kernels for 0% -> 0%
where the time goes in v1:
time: 431 us; the launch traced here: 422 us
  matrix products  150 us (35%)
  blocking collectives  123 us (29%)
  waiting for transfers between devices  50.1 us (12%)
  starting transfers between devices  44.9 us (10%)
  between operations  32.8 us (8%)
  other arithmetic  11.1 us (3%)
  local copies, waits for them, and re-layouts  9.1 us (2%)
    dot_general x8, matrix products, spread(): jnp.dot(row_weights, col_weights, precision=lax.Precision.HIGHEST, prefer...  150 us
    psum x5, blocking collectives, two_products(): lax.psum(lax.psum((jnp.sum(residual * residual), jnp.sum(residual * appli...  62.7 us
    psum x5, blocking collectives, two_products(): lax.psum((jnp.sum(residual * residual), jnp.sum(residual * applied)), ('l...  60.7 us
    ppermute x12, waiting for transfers between devices, extended(): lax.ppermute(lax.slice_in_dim(block, 0, width, axis=dim), axis, backward)  15 us
    ppermute x12, starting transfers between devices, extended(): lax.ppermute(lax.slice_in_dim(block, block.shape[dim] - width, None, axis...  13.8 us
    ppermute x12, starting transfers between devices, extended(): lax.ppermute(lax.slice_in_dim(block, 0, width, axis=dim), axis, backward)  12.9 us
    ppermute x12, waiting for transfers between devices, extended(): lax.ppermute(lax.slice_in_dim(block, block.shape[dim] - width, None, axis...  12.4 us
    all_to_all x1, waiting for transfers between devices, body(): lax.all_to_all(sent_floats.reshape(tile_count, capacity, 3, block_width),...  9.6 us
  transfers between devices with their start and end apart: 29, of which 19 were waited for; matrix products, arithmetic and copies ran while one was open for 2% of the time, Pallas kernels for 0%

profile of v1, /device:TPU:14, one launch (start us, length us, event | category | flops | bytes accessed | tf_op | source)
XLA Modules:
  0.0 422.3 jit_solution(7166894645817641881)
XLA Ops:
  11.3 7.1 %all-to-all-start = ((s32[16,16,128]{2,1,0:T(8,128)}), s32[16,16,128]{2,1,0:T(8,128)S(1)}, u32[]{:S(2)}, u32[]{:S(2)}) async-start(s32[16,16,128]{2,1,0:T(8,128)} %bitcast.5), calls=%async_computation | async-start | bytes 262144 | tf_op jit(solution)/shard_map/all_to_all | solution.py:89
  18.8 4.4 %scatter_fusion = f32[257,3,128]{2,1,0:T(4,128)S(1)} fusion(f32[257,3,128]{2,1,0:T(4,128)S(1)} %broadcast_in_dim.100, s32[128]{0:T(128)S(1)} %fusion.80, f32[128,3,128]{2,1,0:T(4,128)S(1)} %copy.28), kind=kCustom, calls=%fused_computation.1 | custom fusion | bytes 590336 | tf_op jit(solution)/shard_map/scatter | solution.py:77
  24.0 7.0 %all-to-all-start.1 = ((f32[16,16,3,128]{3,1,2,0:T(8,128)}), f32[16,16,3,128]{3,1,2,0:T(8,128)S(1)}, u32[]{:S(2)}, u32[]{:S(2)}) async-start(f32[16,16,3,128]{3,1,2,0:T(8,128)} %copy.29), calls=%async_computation.1 | async-start | bytes 786432 | tf_op jit(solution)/shard_map/all_to_all | solution.py:82
  31.1 9.6 %all-to-all-done.1 = f32[16,16,3,128]{3,1,2,0:T(8,128)S(1)} async-done(((f32[16,16,3,128]{3,1,2,0:T(8,128)}), f32[16,16,3,128]{3,1,2,0:T(8,128)S(1)}, u32[]{:S(2)}, u32[]{:S(2)}) %all-to-all-start.1) | async-done | bytes 393248 | tf_op jit(solution)/shard_map/all_to_all | solution.py:82
  40.9 152.2 %while.16 = (s32[]{:T(128)}, f32[65,1025]{1,0:T(8,128)S(1)}, s32[8,4096]{1,0:T(8,128)S(1)}, f32[8,4096]{1,0:T(8,128)S(1)}, f32[8,4096]{1,0:T(8,128)S(1)}, /*index=5*/f32[8,4096]{1,0:T(8,128)S(1)}, s32[]{:T(128)}, s32[]{:T(128)}) while((s32[]{:T(128)}, f32[65,1025]{1,0:T(8,128)S(1)}, s32[8,4096]{1,0:T(8,128)S(1)}, ...), condition=%wide.region_4.5_spmd.clone.clone, body=%wide.region_3.4_spmd.clone.clone.sunk | while | flops 3297597440 | bytes 942707 | solution.py:135
  41.1 18.8 %fusion.98 = f32[65,1025]{1,0:T(8,128)S(1)} fusion(f32[4096]{0:T(1024)S(1)} %bitcast.58, s32[4096]{0:T(1024)S(1)} %get-tuple-element.322, f32[4096]{0:T(1024)S(1)} %broadcast_subtract_fusion.5, s32[4096]{0:T(1024)S(1)} %get-tuple-element.323, f32[4096]{0:T(1024)S(1)} %bitcast.63, f32[4096]{0:T(1024)S(1)} %bitcast.62, s32[4096]{0:T(1024)S(1)} %bitcast.64, ...), kind=kOutput, calls=%fused_computation.15.clone.1 | convolution fusion | flops 3297474560 | bytes 680457 | tf_op jit(solution)/shard_map/while/body/eval_jaxpr/dot_general | solution.py:126
  60.1 18.8 %fusion.98 = f32[65,1025]{1,0:T(8,128)S(1)} fusion(f32[4096]{0:T(1024)S(1)} %bitcast.58, s32[4096]{0:T(1024)S(1)} %get-tuple-element.322, f32[4096]{0:T(1024)S(1)} %broadcast_subtract_fusion.5, s32[4096]{0:T(1024)S(1)} %get-tuple-element.323, f32[4096]{0:T(1024)S(1)} %bitcast.63, f32[4096]{0:T(1024)S(1)} %bitcast.62, s32[4096]{0:T(1024)S(1)} %bitcast.64, ...), kind=kOutput, calls=%fused_computation.15.clone.1 | convolution fusion | flops 3297474560 | bytes 680457 | tf_op jit(solution)/shard_map/while/body/eval_jaxpr/dot_general | solution.py:126
  79.1 18.8 %fusion.98 = f32[65,1025]{1,0:T(8,128)S(1)} fusion(f32[4096]{0:T(1024)S(1)} %bitcast.58, s32[4096]{0:T(1024)S(1)} %get-tuple-element.322, f32[4096]{0:T(1024)S(1)} %broadcast_subtract_fusion.5, s32[4096]{0:T(1024)S(1)} %get-tuple-element.323, f32[4096]{0:T(1024)S(1)} %bitcast.63, f32[4096]{0:T(1024)S(1)} %bitcast.62, s32[4096]{0:T(1024)S(1)} %bitcast.64, ...), kind=kOutput, calls=%fused_computation.15.clone.1 | convolution fusion | flops 3297474560 | bytes 680457 | tf_op jit(solution)/shard_map/while/body/eval_jaxpr/dot_general | solution.py:126
  98.1 18.8 %fusion.98 = f32[65,1025]{1,0:T(8,128)S(1)} fusion(f32[4096]{0:T(1024)S(1)} %bitcast.58, s32[4096]{0:T(1024)S(1)} %get-tuple-element.322, f32[4096]{0:T(1024)S(1)} %broadcast_subtract_fusion.5, s32[4096]{0:T(1024)S(1)} %get-tuple-element.323, f32[4096]{0:T(1024)S(1)} %bitcast.63, f32[4096]{0:T(1024)S(1)} %bitcast.62, s32[4096]{0:T(1024)S(1)} %bitcast.64, ...), kind=kOutput, calls=%fused_computation.15.clone.1 | convolution fusion | flops 3297474560 | bytes 680457 | tf_op jit(solution)/shard_map/while/body/eval_jaxpr/dot_general | solution.py:126
  117.1 18.8 %fusion.98 = f32[65,1025]{1,0:T(8,128)S(1)} fusion(f32[4096]{0:T(1024)S(1)} %bitcast.58, s32[4096]{0:T(1024)S(1)} %get-tuple-element.322, f32[4096]{0:T(1024)S(1)} %broadcast_subtract_fusion.5, s32[4096]{0:T(1024)S(1)} %get-tuple-element.323, f32[4096]{0:T(1024)S(1)} %bitcast.63, f32[4096]{0:T(1024)S(1)} %bitcast.62, s32[4096]{0:T(1024)S(1)} %bitcast.64, ...), kind=kOutput, calls=%fused_computation.15.clone.1 | convolution fusion | flops 3297474560 | bytes 680457 | tf_op jit(solution)/shard_map/while/body/eval_jaxpr/dot_general | solution.py:126
  136.1 18.8 %fusion.98 = f32[65,1025]{1,0:T(8,128)S(1)} fusion(f32[4096]{0:T(1024)S(1)} %bitcast.58, s32[4096]{0:T(1024)S(1)} %get-tuple-element.322, f32[4096]{0:T(1024)S(1)} %broadcast_subtract_fusion.5, s32[4096]{0:T(1024)S(1)} %get-tuple-element.323, f32[4096]{0:T(1024)S(1)} %bitcast.63, f32[4096]{0:T(1024)S(1)} %bitcast.62, s32[4096]{0:T(1024)S(1)} %bitcast.64, ...), kind=kOutput, calls=%fused_computation.15.clone.1 | convolution fusion | flops 3297474560 | bytes 680457 | tf_op jit(solution)/shard_map/while/body/eval_jaxpr/dot_general | solution.py:126
  155.1 18.8 %fusion.98 = f32[65,1025]{1,0:T(8,128)S(1)} fusion(f32[4096]{0:T(1024)S(1)} %bitcast.58, s32[4096]{0:T(1024)S(1)} %get-tuple-element.322, f32[4096]{0:T(1024)S(1)} %broadcast_subtract_fusion.5, s32[4096]{0:T(1024)S(1)} %get-tuple-element.323, f32[4096]{0:T(1024)S(1)} %bitcast.63, f32[4096]{0:T(1024)S(1)} %bitcast.62, s32[4096]{0:T(1024)S(1)} %bitcast.64, ...), kind=kOutput, calls=%fused_computation.15.clone.1 | convolution fusion | flops 3297474560 | bytes 680457 | tf_op jit(solution)/shard_map/while/body/eval_jaxpr/dot_general | solution.py:126
  174.1 18.8 %fusion.98 = f32[65,1025]{1,0:T(8,128)S(1)} fusion(f32[4096]{0:T(1024)S(1)} %bitcast.58, s32[4096]{0:T(1024)S(1)} %get-tuple-element.322, f32[4096]{0:T(1024)S(1)} %broadcast_subtract_fusion.5, s32[4096]{0:T(1024)S(1)} %get-tuple-element.323, f32[4096]{0:T(1024)S(1)} %bitcast.63, f32[4096]{0:T(1024)S(1)} %bitcast.62, s32[4096]{0:T(1024)S(1)} %bitcast.64, ...), kind=kOutput, calls=%fused_computation.15.clone.1 | convolution fusion | flops 3297474560 | bytes 680457 | tf_op jit(solution)/shard_map/while/body/eval_jaxpr/dot_general | solution.py:126
  204.1 8.9 %reduce-scatter.2.cloned.1.call-done = f32[32,1024]{1,0:T(8,128)} async-done(((f32[64,1024]{1,0:T(8,128)}), f32[32,1024]{1,0:T(8,128)}) %reduce-scatter.2.cloned.1.call-update) | async-done | bytes 131088 | tf_op jit(solution)/shard_map/reduce_scatter | solution.py:145
  226.8 11.2 %all-reduce.4 = (f32[]{:T(128)}, f32[]{:T(128)}) all-reduce(f32[]{:T(128)} %get-tuple-element.194, f32[]{:T(128)} %get-tuple-element.193), channel_id=1, replica_groups=mesh['lat'=4,'lon'=4,'obs'=2] {'lon','obs'}, use_global_device_ids=true, to_apply=%region_8.9 | all-reduce | flops 2 | bytes 16 | tf_op jit(solution)/shard_map/psum | solution.py:41
  238.0 12.3 %all-reduce.9 = (f32[]{:T(128)}, f32[]{:T(128)}) all-reduce(f32[]{:T(128)} %get-tuple-element.215, f32[]{:T(128)} %get-tuple-element.216), channel_id=1, replica_groups=mesh['lat'=4,'lon'=4,'obs'=2] {'lat'}, use_global_device_ids=true, to_apply=%region_9.10 | all-reduce | flops 2 | bytes 16 | tf_op jit(solution)/shard_map/psum | solution.py:40
  262.9 11.6 %all-reduce.3 = (f32[]{:T(128)}, f32[]{:T(128)}) all-reduce(f32[]{:T(128)} %get-tuple-element.192, f32[]{:T(128)} %get-tuple-element.191), channel_id=1, replica_groups=mesh['lat'=4,'lon'=4,'obs'=2] {'lon','obs'}, use_global_device_ids=true, to_apply=%region_14.15 | all-reduce | flops 2 | bytes 16 | tf_op jit(solution)/shard_map/psum | solution.py:41
  274.5 12.6 %all-reduce.8 = (f32[]{:T(128)}, f32[]{:T(128)}) all-reduce(f32[]{:T(128)} %get-tuple-element.213, f32[]{:T(128)} %get-tuple-element.214), channel_id=1, replica_groups=mesh['lat'=4,'lon'=4,'obs'=2] {'lat'}, use_global_device_ids=true, to_apply=%region_15.16 | all-reduce | flops 2 | bytes 16 | tf_op jit(solution)/shard_map/psum | solution.py:40
  303.5 12.6 %all-reduce.2 = (f32[]{:T(128)}, f32[]{:T(128)}) all-reduce(f32[]{:T(128)} %get-tuple-element.190, f32[]{:T(128)} %get-tuple-element.189), channel_id=1, replica_groups=mesh['lat'=4,'lon'=4,'obs'=2] {'lon','obs'}, use_global_device_ids=true, to_apply=%region_20.21 | all-reduce | flops 2 | bytes 16 | tf_op jit(solution)/shard_map/psum | solution.py:41
  316.1 12.6 %all-reduce.7 = (f32[]{:T(128)}, f32[]{:T(128)}) all-reduce(f32[]{:T(128)} %get-tuple-element.211, f32[]{:T(128)} %get-tuple-element.212), channel_id=1, replica_groups=mesh['lat'=4,'lon'=4,'obs'=2] {'lat'}, use_global_device_ids=true, to_apply=%region_21.22 | all-reduce | flops 2 | bytes 16 | tf_op jit(solution)/shard_map/psum | solution.py:40
  344.5 12.6 %all-reduce.1 = (f32[]{:T(128)}, f32[]{:T(128)}) all-reduce(f32[]{:T(128)} %get-tuple-element.188, f32[]{:T(128)} %get-tuple-element.187), channel_id=1, replica_groups=mesh['lat'=4,'lon'=4,'obs'=2] {'lon','obs'}, use_global_device_ids=true, to_apply=%region_26.27 | all-reduce | flops 2 | bytes 16 | tf_op jit(solution)/shard_map/psum | solution.py:41
  357.1 12.6 %all-reduce.6 = (f32[]{:T(128)}, f32[]{:T(128)}) all-reduce(f32[]{:T(128)} %get-tuple-element.209, f32[]{:T(128)} %get-tuple-element.210), channel_id=1, replica_groups=mesh['lat'=4,'lon'=4,'obs'=2] {'lat'}, use_global_device_ids=true, to_apply=%region_27.28 | all-reduce | flops 2 | bytes 16 | tf_op jit(solution)/shard_map/psum | solution.py:40
  385.5 12.6 %all-reduce = (f32[]{:T(128)}, f32[]{:T(128)}) all-reduce(f32[]{:T(128)} %get-tuple-element.186, f32[]{:T(128)} %get-tuple-element.185), channel_id=1, replica_groups=mesh['lat'=4,'lon'=4,'obs'=2] {'lon','obs'}, use_global_device_ids=true, to_apply=%region_32.33 | all-reduce | flops 2 | bytes 16 | tf_op jit(solution)/shard_map/psum | solution.py:41
  398.1 12.6 %all-reduce.5 = (f32[]{:T(128)}, f32[]{:T(128)}) all-reduce(f32[]{:T(128)} %get-tuple-element.207, f32[]{:T(128)} %get-tuple-element.208), channel_id=1, replica_groups=mesh['lat'=4,'lon'=4,'obs'=2] {'lat'}, use_global_device_ids=true, to_apply=%region_33.34 | all-reduce | flops 2 | bytes 16 | tf_op jit(solution)/shard_map/psum | solution.py:40
  (162 shorter events, 78.2 us)
Async XLA Ops:
  11.3 12.7 %all-to-all-start = ((s32[16,16,128]{2,1,0:T(8,128)}), s32[16,16,128]{2,1,0:T(8,128)S(1)}, u32[]{:S(2)}, u32[]{:S(2)}) async-start(s32[16,16,128]{2,1,0:T(8,128)} %bitcast.5), calls=%async_computation | async-start | bytes 262144 | tf_op jit(solution)/shard_map/all_to_all | solution.py:89
  24.0 16.7 %all-to-all-start.1 = ((f32[16,16,3,128]{3,1,2,0:T(8,128)}), f32[16,16,3,128]{3,1,2,0:T(8,128)S(1)}, u32[]{:S(2)}, u32[]{:S(2)}) async-start(f32[16,16,3,128]{3,1,2,0:T(8,128)} %copy.29), calls=%async_computation.1 | async-start | bytes 786432 | tf_op jit(solution)/shard_map/all_to_all | solution.py:82
  31.0 182.0 %reduce-scatter.2.cloned.1.call-start = ((), (), s32[]{:S(2)}) async-start(), calls=%async_computation.3 | async-start | bytes 393216 | tf_op jit(solution)/shard_map/reduce_scatter | solution.py:145
  193.2 3.6 collective-permute-start
  197.8 5.5 %collective-permute-start.1 = (f32[1024]{0:T(1024)S(1)}, f32[1024]{0:T(1024)S(1)}, u32[]{:S(2)}, u32[]{:S(2)}) collective-permute-start(f32[1024]{0:T(1024)S(1)} %bitcast.68), channel_id=1, source_target_pairs={{0,8},{8,16},{16,24},{1,9},{9,17},{17,25},{2,10},{10,18},{18,26},{... | collective-permute-start | bytes 12296 | tf_op jit(solution)/shard_map/ppermute | solution.py:32
  214.0 3.6 collective-permute-start.2
  214.4 3.2 collective-permute-start.3
  215.8 3.9 collective-permute-start.6
  215.8 3.9 collective-permute-start.7
  217.7 4.1 collective-permute-start.4
  218.2 4.8 %collective-permute-start.5 = (f32[34,1]{1,0:T(8,128)S(1)}, f32[34,1]{1,0:T(8,128)S(1)}, u32[]{:S(2)}, u32[]{:S(2)}) collective-permute-start(f32[34,1]{1,0:T(8,128)S(1)} %get-tuple-element.254), channel_id=1, source_target_pairs={{2,0},{4,2},{6,4},{0,6},{3,1},{5,3},{7,5},{1,7},{10,8},{12,10},{14... | collective-permute-start | bytes 416 | tf_op jit(solution)/shard_map/ppermute | solution.py:18
  219.8 3.8 collective-permute-start.8
  221.2 4.7 %collective-permute-start.9 = (f32[34,1]{1,0:T(8,128)S(1)}, f32[34,1]{1,0:T(8,128)S(1)}, u32[]{:S(2)}, u32[]{:S(2)}) collective-permute-start(f32[34,1]{1,0:T(8,128)S(1)} %get-tuple-element.256), channel_id=1, source_target_pairs={{2,0},{4,2},{6,4},{0,6},{3,1},{5,3},{7,5},{1,7},{10,8},{12,10},{14... | collective-permute-start | bytes 416 | tf_op jit(solution)/shard_map/ppermute | solution.py:18
  251.7 3.1 collective-permute-start.10
  254.9 3.8 collective-permute-start.12
  257.1 4.8 %collective-permute-start.13 = (f32[34,1]{1,0:T(8,128)S(1)}, f32[34,1]{1,0:T(8,128)S(1)}, u32[]{:S(2)}, u32[]{:S(2)}) collective-permute-start(f32[34,1]{1,0:T(8,128)S(1)} %get-tuple-element.252), channel_id=1, source_target_pairs={{2,0},{4,2},{6,4},{0,6},{3,1},{5,3},{7,5},{1,7},{10,8},{12,10},{14... | collective-permute-start | bytes 416 | tf_op jit(solution)/shard_map/ppermute | solution.py:18
  291.7 3.1 collective-permute-start.14
  294.9 4.9 %collective-permute-start.16 = (f32[34,1]{1,0:T(8,128)S(1)}, f32[34,1]{1,0:T(8,128)S(1)}, u32[]{:S(2)}, u32[]{:S(2)}) collective-permute-start(f32[34,1]{1,0:T(8,128)S(1)} %get-tuple-element.249), channel_id=1, source_target_pairs={{0,2},{2,4},{4,6},{6,0},{1,3},{3,5},{5,7},{7,1},{8,10},{10,12},{12... | collective-permute-start | bytes 416 | tf_op jit(solution)/shard_map/ppermute | solution.py:15
  297.9 4.7 %collective-permute-start.17 = (f32[34,1]{1,0:T(8,128)S(1)}, f32[34,1]{1,0:T(8,128)S(1)}, u32[]{:S(2)}, u32[]{:S(2)}) collective-permute-start(f32[34,1]{1,0:T(8,128)S(1)} %get-tuple-element.250), channel_id=1, source_target_pairs={{2,0},{4,2},{6,4},{0,6},{3,1},{5,3},{7,5},{1,7},{10,8},{12,10},{14... | collective-permute-start | bytes 416 | tf_op jit(solution)/shard_map/ppermute | solution.py:18
  332.7 3.1 collective-permute-start.18
  335.9 4.9 %collective-permute-start.20 = (f32[34,1]{1,0:T(8,128)S(1)}, f32[34,1]{1,0:T(8,128)S(1)}, u32[]{:S(2)}, u32[]{:S(2)}) collective-permute-start(f32[34,1]{1,0:T(8,128)S(1)} %get-tuple-element.247), channel_id=1, source_target_pairs={{0,2},{2,4},{4,6},{6,0},{1,3},{3,5},{5,7},{7,1},{8,10},{10,12},{12... | collective-permute-start | bytes 416 | tf_op jit(solution)/shard_map/ppermute | solution.py:15
  338.9 4.7 %collective-permute-start.21 = (f32[34,1]{1,0:T(8,128)S(1)}, f32[34,1]{1,0:T(8,128)S(1)}, u32[]{:S(2)}, u32[]{:S(2)}) collective-permute-start(f32[34,1]{1,0:T(8,128)S(1)} %get-tuple-element.248), channel_id=1, source_target_pairs={{2,0},{4,2},{6,4},{0,6},{3,1},{5,3},{7,5},{1,7},{10,8},{12,10},{14... | collective-permute-start | bytes 416 | tf_op jit(solution)/shard_map/ppermute | solution.py:18
  376.9 4.9 %collective-permute-start.24 = (f32[34,1]{1,0:T(8,128)S(1)}, f32[34,1]{1,0:T(8,128)S(1)}, u32[]{:S(2)}, u32[]{:S(2)}) collective-permute-start(f32[34,1]{1,0:T(8,128)S(1)} %get-tuple-element.245), channel_id=1, source_target_pairs={{0,2},{2,4},{4,6},{6,0},{1,3},{3,5},{5,7},{7,1},{8,10},{10,12},{12... | collective-permute-start | bytes 416 | tf_op jit(solution)/shard_map/ppermute | solution.py:15
  379.9 4.7 %collective-permute-start.25 = (f32[34,1]{1,0:T(8,128)S(1)}, f32[34,1]{1,0:T(8,128)S(1)}, u32[]{:S(2)}, u32[]{:S(2)}) collective-permute-start(f32[34,1]{1,0:T(8,128)S(1)} %get-tuple-element.246), channel_id=1, source_target_pairs={{2,0},{4,2},{6,4},{0,6},{3,1},{5,3},{7,5},{1,7},{10,8},{12,10},{14... | collective-permute-start | bytes 416 | tf_op jit(solution)/shard_map/ppermute | solution.py:18
  (12 other events, 105.5 us)
Sparse Core Ops, SparseCore 0:
  204.2 8.7 reduce-scatter.1
